TPU v7x, 32 devices: a whole 2x2x4 slice. The times are simulated.
32 devices in a mesh: rows: 8 (over z, x), rep: 4 (over y, core).
Axes of the slice: x: 2, y: 2, z: 4, core: 2. Of those that a mesh axis runs over, the one named last changes fastest.
Arguments:
- requests: int32 [32, 8, 128], P(('rows', 'rep')), may hold values from 0 to 1023
- request_counts: int32 [32, 8], P(('rows', 'rep')), may hold values from 0 to 128, as said below
- table: bfloat16 [8192, 512], P('rows')
- gain: float32 [512], replicated, may hold values from 0.5 to 1.5
Outputs:
- normalized: bfloat16 [32, 8, 128, 512], P(('rows', 'rep'))
- row_counts: int32 [8192], P('rows')
- moments: float32 [2, 2], replicated
Inputs may be any that keep to these rules, and one draw needn't show every extreme that they name: Each device uses request_counts[d, o] of its 128 slots toward owner o; in every draw one owner's slots are full from every device.
All inputs are finite; a program needn't handle non-finite values.
Results may differ from a plain program's by a relative error of at most 0.0004.
Values may be sent and summed in bfloat16 or wider, within the bound.
No kernel may reach another device: no remote copies, remote signals or barrier semaphores. Data moves between devices by JAX's collectives and lax.ppermute only.
A program may use at most 64 MiB of HBM per device.

v0:
```python
import jax
import jax.numpy as jnp
from jax import lax
from jax.sharding import PartitionSpec as P

WIDTH = 256
LAYERS = 2
epsilon = 1e-06


def joined(part, axis, combine):
    gathered = jax.tree.map(lambda a: lax.all_gather(a, axis), part)

    def take(source):
        return jax.tree.map(lambda a: lax.dynamic_index_in_dim(a, source, 0, False), gathered)

    return lax.fori_loop(
        1, lax.axis_size(axis), lambda source, state: combine(state, take(source)), take(0)
    )


def merge_moments(former, latter):
    count_former, mean_former, square_former = former
    count_latter, mean_latter, square_latter = latter
    merged_count = count_former + count_latter
    safe_count = jnp.maximum(merged_count, 1.0)
    delta_mean = mean_latter - mean_former
    merged_mean = mean_former + delta_mean * count_latter / safe_count
    merged_square = (
        square_former
        + square_latter
        + delta_mean * delta_mean * count_former * count_latter / safe_count
    )
    return (merged_count, merged_mean, merged_square)


def per_device(requests, request_counts, table, gain):
    wanted, wanted_counts = (
        lax.all_to_all(requests, "rows", split_axis=1, concat_axis=0, tiled=True),
        lax.all_to_all(request_counts, "rows", split_axis=1, concat_axis=0, tiled=True),
    )
    owners = wanted.shape[0]
    slot_count = wanted.shape[2]
    held_rows = table.shape[0]
    row_index = wanted.reshape(-1)
    live_slot = lax.broadcasted_iota(jnp.int32, (owners, slot_count), 1) < wanted_counts
    live_flat = live_slot.reshape(-1)
    matches = (row_index[:, None] == jnp.arange(held_rows, dtype=jnp.int32)[None, :]) & live_flat[
        :, None
    ]
    local_counts = jnp.sum(matches.astype(jnp.int32), axis=0)
    row_counts = lax.psum(local_counts, "rep")
    shaped = table.reshape(held_rows, LAYERS, WIDTH)
    weights = row_counts.astype(jnp.float32)
    partial_value = jnp.dot(
        weights, jnp.sum(shaped, axis=2, dtype=jnp.float32), precision=lax.Precision.HIGHEST
    )
    count_layers = jnp.full((LAYERS,), jnp.sum(weights) * WIDTH, jnp.float32)
    mean_here = partial_value / jnp.maximum(count_layers, 1.0)
    centered = jnp.sum(jnp.square(shaped.astype(jnp.float32) - mean_here[None, :, None]), axis=2)
    square_here = jnp.dot(weights, centered, precision=lax.Precision.HIGHEST)
    entries, layer_mean, merged_square = joined(
        (count_layers, mean_here, square_here), "rows", merge_moments
    )
    layer_var = merged_square / entries
    inverse = jnp.repeat(lax.rsqrt(layer_var + epsilon), WIDTH) * gain
    mean_full = jnp.repeat(layer_mean, WIDTH)
    looked = jnp.take(table, row_index, axis=0).reshape(owners, 1, slot_count, LAYERS * WIDTH)
    scaled = (looked.astype(jnp.float32) - mean_full) * inverse
    scaled = jnp.where(live_slot.reshape(owners, 1, slot_count, 1), scaled, 0.0).astype(
        jnp.bfloat16
    )
    normalized = lax.all_to_all(scaled, "rows", split_axis=0, concat_axis=1, tiled=True)
    return (normalized, row_counts, jnp.stack([layer_mean, layer_var]))


def solution(mesh):
    return jax.shard_map(
        per_device,
        mesh=mesh,
        in_specs=(P(("rows", "rep"), None, None), P(("rows", "rep"), None), P("rows", None), P()),
        out_specs=(P(("rows", "rep"), None, None, None), P("rows"), P()),
        check_vma=False,
    )
```

profile of v0, /device:TPU:0, one launch (start us, length us, event | category | flops | bytes accessed | tf_op | source)
XLA Modules:
  0.0 89.4 jit_solution(5345991908360352691)
XLA Ops:
  0.6 1.3 %copy.13 = s32[1,8,1]{2,0,1:T(1,128)} copy(s32[1,8,1]{1,2,0:T(1,128)} %bitcast.86) | data formatting | bytes 64 | tf_op jit(solution)/shard_map/all_to_all | solution.py:40
  2.0 7.3 %all-to-all-start = ((s32[1,8,1]{2,0,1:T(1,128)}), s32[1,8,1]{2,0,1:T(1,128)S(1)}, u32[]{:S(2)}, u32[]{:S(2)}) async-start(s32[1,8,1]{2,0,1:T(1,128)} %copy.13), calls=%async_computation | async-start | bytes 8192 | tf_op jit(solution)/shard_map/all_to_all | solution.py:40
  9.2 2.4 %reshape.157 = f32[1024,2,256]{2,1,0:T(2,128)S(1)} reshape(bf16[1024,512]{1,0:T(8,128)(2,1)} %param.8) | data formatting | bytes 3145728 | tf_op jit(solution)/shard_map/convert_element_type | solution.py:56
  11.6 0.0 copy-start.3
  11.6 1.9 %reduce_sum.38 = f32[1024,2]{1,0:T(8,128)} reduce(f32[1024,2,256]{2,1,0:T(2,128)S(1)} %reshape.157, f32[]{:T(128)} %constant.79.clone.1), dimensions={2}, to_apply=%region_3.0 | reduce | flops 522240 | bytes 2105348 | tf_op jit(solution)/shard_map/reduce_sum | solution.py:56
  13.6 0.0 copy-start
  13.6 0.0 copy-done.3
  13.6 0.7 dynamic-slice
  14.9 0.7 all-to-all-done
  15.7 5.3 %all-to-all-start.1 = ((s32[1,8,128]{2,0,1:T(1,128)}), s32[1,8,128]{2,0,1:T(1,128)S(1)}, u32[]{:S(2)}, u32[]{:S(2)}) async-start(s32[1,8,128]{2,0,1:T(1,128)} %bitcast.4), calls=%async_computation.1 | async-start | bytes 8192 | tf_op jit(solution)/shard_map/all_to_all | solution.py:39
  20.9 0.2 reduce
  21.2 0.1 iota_compare_fusion.1
  21.3 6.1 %all-to-all-done.1 = s32[1,8,128]{2,0,1:T(1,128)S(1)} async-done(((s32[1,8,128]{2,0,1:T(1,128)}), s32[1,8,128]{2,0,1:T(1,128)S(1)}, u32[]{:S(2)}, u32[]{:S(2)}) %all-to-all-start.1) | async-done | bytes 4128 | tf_op jit(solution)/shard_map/all_to_all | solution.py:39
  27.4 0.8 convert_reduce_fusion
  28.1 5.0 %psum.7 = s32[1024]{0:T(1024)S(1)} all-reduce(s32[1024]{0:T(1024)S(1)} %convert_reduce_fusion), channel_id=1, replica_groups=mesh['rows'=8,'rep'=4] {'rep'}, use_global_device_ids=true, to_apply=%region_1.0 | all-reduce | flops 1024 | bytes 8192 | tf_op jit(solution)/shard_map/psum | solution.py:52
  33.1 0.0 copy-start.1
  33.1 0.6 convert_reduce_fusion.1
  34.4 1.4 %fusion.8 = f32[2]{0:T(128)S(1)} fusion(f32[1024,1]{0,1:T(1,128)S(1)} %bitcast.77, f32[1024,2]{1,0:T(8,128)} %reduce_sum.38, f32[]{:T(128)S(6)} %max.14), kind=kOutput, calls=%fused_computation.19 | convolution fusion | flops 24578 | bytes 12300 | tf_op jit(solution)/shard_map/dot_general | solution.py:55
  35.8 1.3 %multiply_reduce_fusion = f32[1024,2]{1,0:T(8,128)S(1)} fusion(f32[1024,2,256]{2,1,0:T(2,128)S(1)} %reshape.157, f32[2]{0:T(128)S(1)} %fusion.8), kind=kLoop, calls=%fused_computation.16 | loop fusion | flops 1570816 | bytes 2105352 | tf_op jit(solution)/shard_map/reduce_sum | solution.py:60
  37.0 0.4 convolution_bitcast_fusion
  37.4 0.2 dynamic-update-slice.1
  37.6 0.2 dynamic-update-slice.2
  37.8 0.8 dynamic-update-slice
  38.6 17.7 %all-reduce.3 = (f32[8]{0:T(128)S(1)}, f32[16]{0:T(128)S(1)}, f32[16]{0:T(128)S(1)}) all-reduce(f32[8]{0:T(128)S(1)} %dynamic-update-slice, f32[16]{0:T(128)S(1)} %dynamic-update-slice.1, f32[16]{0:T(128)S(1)} %dynamic-update-slice.2), channel_id=2, replica_groups=mesh['rows'=8,'rep'=4] {'rows'}, use_global_device_ids=true, to_apply=%add | all-reduce | flops 40 | bytes 320
  56.3 0.1 reshape.168
  56.4 0.1 reshape.169
  56.5 0.1 broadcast.115
  56.6 0.5 while.19
  57.1 0.1 broadcast_bitcast_fusion
  57.2 0.1 broadcast_bitcast_fusion.1
  57.3 0.0 copy-done
  57.3 0.0 copy-start.2
  57.3 4.0 %gather_fusion = bf16[1024,512]{1,0:T(8,128)(2,1)S(1)} fusion(bf16[1024,512]{1,0:T(8,128)(2,1)S(1)} %copy-done, s32[1024]{0:T(1024)S(1)} %broadcast_clamp_fusion), kind=kCustom, calls=%fused_computation | custom fusion | bytes 2101248 | tf_op jit(solution)/shard_map/jit(_take)/gather | solution.py:68
  61.3 0.0 copy-done.1
  61.3 0.0 copy-done.2
  61.3 1.8 %select_convert_fusion = bf16[8,1,128,512]{3,2,1,0:T(8,128)(2,1)} fusion(f32[512]{0:T(512)S(1)} %mul.63, f32[512]{0:T(512)S(1)} %bitcast.83, bf16[8,1,128,512]{3,2,1,0:T(8,128)(2,1)S(1)} %bitcast.73, pred[8,128]{1,0:T(8,128)(4,1)S(1)} %compare_and_fusion, pred[8,128]{1,0:T(8,128)(4,1)S(1)} %get-tuple-element.205), kind=kLoop, calls=%fused_computation.15 | loop fusion | flops 3145728 | bytes 2103296 | tf_op jit(solution)/shard_map/convert_element_type | solution.py:70
  63.1 3.6 %all-to-all-start.2 = ((bf16[8,1,128,512]{3,2,1,0:T(8,128)(2,1)}), bf16[8,1,128,512]{3,2,1,0:T(8,128)(2,1)S(1)}, u32[]{:S(2)}, u32[]{:S(2)}) async-start(bf16[8,1,128,512]{3,2,1,0:T(8,128)(2,1)} %select_convert_fusion), calls=%async_computation.2 | async-start | bytes 2097152 | tf_op jit(solution)/shard_map/all_to_all | solution.py:73
  66.6 0.6 pad_maximum_fusion
  67.2 21.2 %all-to-all-done.2 = bf16[8,1,128,512]{3,2,1,0:T(8,128)(2,1)S(1)} async-done(((bf16[8,1,128,512]{3,2,1,0:T(8,128)(2,1)}), bf16[8,1,128,512]{3,2,1,0:T(8,128)(2,1)S(1)}, u32[]{:S(2)}, u32[]{:S(2)}) %all-to-all-start.2) | async-done | bytes 1048608 | tf_op jit(solution)/shard_map/all_to_all | solution.py:73
  88.4 1.0 %copy.35 = bf16[1,8,128,512]{3,2,1,0:T(8,128)(2,1)} copy(bf16[1,8,128,512]{3,2,1,0:T(8,128)(2,1)S(1)} %bitcast.74) | data formatting | bytes 2097152
  (26 shorter events, 0.4 us)
Async XLA Ops:
  2.0 13.7 %all-to-all-start = ((s32[1,8,1]{2,0,1:T(1,128)}), s32[1,8,1]{2,0,1:T(1,128)S(1)}, u32[]{:S(2)}, u32[]{:S(2)}) async-start(s32[1,8,1]{2,0,1:T(1,128)} %copy.13), calls=%async_computation | async-start | bytes 8192 | tf_op jit(solution)/shard_map/all_to_all | solution.py:40
  11.6 2.0 %copy-start.3 = (u32[32]{0:T(128)S(1)}, u32[32]{0:T(128)}, u32[]{:S(2)}) copy-start(u32[32]{0:T(128)} %constant.87) | copy-start | bytes 388
  13.6 43.7 %copy-start = (bf16[1024,512]{1,0:T(8,128)(2,1)S(1)}, bf16[1024,512]{1,0:T(8,128)(2,1)}, u32[]{:S(2)}) copy-start(bf16[1024,512]{1,0:T(8,128)(2,1)} %param.8) | copy-start | bytes 3145732
  15.7 11.7 %all-to-all-start.1 = ((s32[1,8,128]{2,0,1:T(1,128)}), s32[1,8,128]{2,0,1:T(1,128)S(1)}, u32[]{:S(2)}, u32[]{:S(2)}) async-start(s32[1,8,128]{2,0,1:T(1,128)} %bitcast.4), calls=%async_computation.1 | async-start | bytes 8192 | tf_op jit(solution)/shard_map/all_to_all | solution.py:39
  33.1 28.2 %copy-start.1 = (s32[1024]{0:T(1024)}, s32[1024]{0:T(1024)S(1)}, u32[]{:S(2)}) copy-start(s32[1024]{0:T(1024)S(1)} %psum.7) | copy-start | bytes 12292
  57.3 4.0 %copy-start.2 = (f32[512]{0:T(512)S(1)}, f32[512]{0:T(512)}, u32[]{:S(2)}) copy-start(f32[512]{0:T(512)} %param.9) | copy-start | bytes 6148
  63.1 25.4 %all-to-all-start.2 = ((bf16[8,1,128,512]{3,2,1,0:T(8,128)(2,1)}), bf16[8,1,128,512]{3,2,1,0:T(8,128)(2,1)S(1)}, u32[]{:S(2)}, u32[]{:S(2)}) async-start(bf16[8,1,128,512]{3,2,1,0:T(8,128)(2,1)} %select_convert_fusion), calls=%async_computation.2 | async-start | bytes 2097152 | tf_op jit(solution)/shard_map/all_to_all | solution.py:73
where the time goes:
time: 89.8 us; the launch traced here: 89.4 us
  waiting for transfers between devices  28.1 us (31%)
  blocking collectives  22.6 us (25%)
  starting transfers between devices  16.1 us (18%)
  local copies, waits for them, and re-layouts  11 us (12%)
  other arithmetic  7.57 us (8%)
  between operations  2.13 us (2%)
  matrix products  1.75 us (2%)
    all_to_all x1, waiting for transfers between devices, per_device(): lax.all_to_all(scaled, 'rows', split_axis=0, concat_axis=1, tiled=True)  21.2 us
    unnamed x1, blocking collectives  17.7 us
    all_to_all x1, starting transfers between devices, per_device(): lax.all_to_all(request_counts, 'rows', split_axis=1, concat_axis=0, tiled...  7.28 us
    all_to_all x1, waiting for transfers between devices, per_device(): lax.all_to_all(requests, 'rows', split_axis=1, concat_axis=0, tiled=True)  6.11 us
    all_to_all x1, starting transfers between devices, per_device(): lax.all_to_all(requests, 'rows', split_axis=1, concat_axis=0, tiled=True)  5.29 us
    psum x1, blocking collectives, per_device(): row_counts = lax.psum(local_counts, 'rep')  4.97 us
    gather x1, local copies, waits for them, and re-layouts, per_device(): jnp.take(table, row_index, axis=0)  3.97 us
    all_to_all x1, starting transfers between devices, per_device(): lax.all_to_all(scaled, 'rows', split_axis=0, concat_axis=1, tiled=True)  3.56 us
  transfers between devices with their start and end apart: 3, of which 3 were waited for; matrix products, arithmetic and copies ran while one was open for 7% of the time, Pallas kernels for 0%

commit v1 on v0

--- a/solution.py
+++ b/solution.py
@@ -70,7 +70,10 @@
     scaled = jnp.where(live_slot.reshape(owners, 1, slot_count, 1), scaled, 0.0).astype(
         jnp.bfloat16
     )
-    normalized = lax.all_to_all(scaled, "rows", split_axis=0, concat_axis=1, tiled=True)
+    count = lax.axis_size("rows")
+    blocks = jnp.stack(jnp.split(scaled, count, axis=0), axis=0)
+    blocks = lax.all_to_all(blocks, "rows", split_axis=0, concat_axis=0)
+    normalized = jnp.concatenate(blocks, axis=1)
     return (normalized, row_counts, jnp.stack([layer_mean, layer_var]))
 
 

time: 89.8 us -> 94.3 us (1.050)
  local copies, waits for them, and re-layouts: 11 us -> 16.3 us
    unnamed x21 -> x28, local copies, waits for them, and re-layouts: 3.12 us -> 7.77 us
  transfers between devices with their start and end apart: 3 -> 3, of which waited for: 3 -> 3; matrix products, arithmetic and copies ran while one was open for 7% -> 6% of each run, Pallas kernels for 0% -> 0%
where the time goes in v1:
time: 94.3 us; the launch traced here: 93.9 us
  waiting for transfers between devices  28.1 us (30%)
  blocking collectives  22.6 us (24%)
  local copies, waits for them, and re-layouts  16.3 us (17%)
  starting transfers between devices  16.1 us (17%)
  other arithmetic  6.78 us (7%)
  between operations  2.14 us (2%)
  matrix products  1.75 us (2%)
    all_to_all x1, waiting for transfers between devices, per_device(): blocks = lax.all_to_all(blocks, 'rows', split_axis=0, concat_axis=0)  21.2 us
    unnamed x1, blocking collectives  17.7 us
    unnamed x28, local copies, waits for them, and re-layouts  7.77 us
    all_to_all x1, starting transfers between devices, per_device(): lax.all_to_all(request_counts, 'rows', split_axis=1, concat_axis=0, tiled...  7.28 us
    all_to_all x1, waiting for transfers between devices, per_device(): lax.all_to_all(requests, 'rows', split_axis=1, concat_axis=0, tiled=True)  6.11 us
    all_to_all x1, starting transfers between devices, per_device(): lax.all_to_all(requests, 'rows', split_axis=1, concat_axis=0, tiled=True)  5.29 us
    psum x1, blocking collectives, per_device(): row_counts = lax.psum(local_counts, 'rep')  4.97 us
    gather x1, local copies, waits for them, and re-layouts, per_device(): jnp.take(table, row_index, axis=0)  3.97 us
  transfers between devices with their start and end apart: 3, of which 3 were waited for; matrix products, arithmetic and copies ran while one was open for 6% of the time, Pallas kernels for 0%

profile of v1, /device:TPU:0, one launch (start us, length us, event | category | flops | bytes accessed | tf_op | source)
XLA Modules:
  0.0 93.9 jit_solution(3397284827078001502)
XLA Ops:
  0.6 1.3 %copy.29 = s32[1,8,1]{2,0,1:T(1,128)} copy(s32[1,8,1]{1,2,0:T(1,128)} %bitcast.118) | data formatting | bytes 64 | tf_op jit(solution)/shard_map/all_to_all | solution.py:40
  2.0 7.3 %all-to-all-start = ((s32[1,8,1]{2,0,1:T(1,128)}), s32[1,8,1]{2,0,1:T(1,128)S(1)}, u32[]{:S(2)}, u32[]{:S(2)}) async-start(s32[1,8,1]{2,0,1:T(1,128)} %copy.29), calls=%async_computation | async-start | bytes 8192 | tf_op jit(solution)/shard_map/all_to_all | solution.py:40
  9.2 2.4 %reshape.158 = f32[1024,2,256]{2,1,0:T(2,128)S(1)} reshape(bf16[1024,512]{1,0:T(8,128)(2,1)} %param.8) | data formatting | bytes 3145728 | tf_op jit(solution)/shard_map/convert_element_type | solution.py:56
  11.6 0.0 copy-start.3
  11.6 1.9 %reduce_sum.38 = f32[1024,2]{1,0:T(8,128)} reduce(f32[1024,2,256]{2,1,0:T(2,128)S(1)} %reshape.158, f32[]{:T(128)} %constant.79.clone.1), dimensions={2}, to_apply=%region_3.0 | reduce | flops 522240 | bytes 2105348 | tf_op jit(solution)/shard_map/reduce_sum | solution.py:56
  13.6 0.0 copy-start
  13.6 0.0 copy-done.3
  13.6 0.7 dynamic-slice
  14.9 0.7 all-to-all-done
  15.7 5.3 %all-to-all-start.1 = ((s32[1,8,128]{2,0,1:T(1,128)}), s32[1,8,128]{2,0,1:T(1,128)S(1)}, u32[]{:S(2)}, u32[]{:S(2)}) async-start(s32[1,8,128]{2,0,1:T(1,128)} %bitcast.4), calls=%async_computation.1 | async-start | bytes 8192 | tf_op jit(solution)/shard_map/all_to_all | solution.py:39
  20.9 0.2 reduce
  21.2 0.1 iota_compare_fusion.1
  21.3 6.1 %all-to-all-done.1 = s32[1,8,128]{2,0,1:T(1,128)S(1)} async-done(((s32[1,8,128]{2,0,1:T(1,128)}), s32[1,8,128]{2,0,1:T(1,128)S(1)}, u32[]{:S(2)}, u32[]{:S(2)}) %all-to-all-start.1) | async-done | bytes 4128 | tf_op jit(solution)/shard_map/all_to_all | solution.py:39
  27.4 0.8 convert_reduce_fusion
  28.1 5.0 %psum.7 = s32[1024]{0:T(1024)S(1)} all-reduce(s32[1024]{0:T(1024)S(1)} %convert_reduce_fusion), channel_id=1, replica_groups=mesh['rows'=8,'rep'=4] {'rep'}, use_global_device_ids=true, to_apply=%region_1.0 | all-reduce | flops 1024 | bytes 8192 | tf_op jit(solution)/shard_map/psum | solution.py:52
  33.1 0.0 copy-start.1
  33.1 0.6 convert_reduce_fusion.1
  34.4 1.4 %fusion.8 = f32[2]{0:T(128)S(1)} fusion(f32[1024,1]{0,1:T(1,128)S(1)} %bitcast.109, f32[1024,2]{1,0:T(8,128)} %reduce_sum.38, f32[]{:T(128)S(6)} %max.14), kind=kOutput, calls=%fused_computation.19 | convolution fusion | flops 24578 | bytes 12300 | tf_op jit(solution)/shard_map/dot_general | solution.py:55
  35.8 1.3 %multiply_reduce_fusion = f32[1024,2]{1,0:T(8,128)S(1)} fusion(f32[1024,2,256]{2,1,0:T(2,128)S(1)} %reshape.158, f32[2]{0:T(128)S(1)} %fusion.8), kind=kLoop, calls=%fused_computation.16 | loop fusion | flops 1570816 | bytes 2105352 | tf_op jit(solution)/shard_map/reduce_sum | solution.py:60
  37.0 0.4 convolution_bitcast_fusion
  37.4 0.2 dynamic-update-slice.1
  37.6 0.2 dynamic-update-slice.2
  37.8 0.8 dynamic-update-slice
  38.6 17.7 %all-reduce.3 = (f32[8]{0:T(128)S(1)}, f32[16]{0:T(128)S(1)}, f32[16]{0:T(128)S(1)}) all-reduce(f32[8]{0:T(128)S(1)} %dynamic-update-slice, f32[16]{0:T(128)S(1)} %dynamic-update-slice.1, f32[16]{0:T(128)S(1)} %dynamic-update-slice.2), channel_id=2, replica_groups=mesh['rows'=8,'rep'=4] {'rows'}, use_global_device_ids=true, to_apply=%add | all-reduce | flops 40 | bytes 320
  56.3 0.1 reshape.169
  56.4 0.1 reshape.170
  56.5 0.1 broadcast.115
  56.6 0.5 while.19
  57.1 0.1 broadcast_bitcast_fusion
  57.2 0.1 broadcast_bitcast_fusion.1
  57.3 0.0 copy-done
  57.3 0.0 copy-start.2
  57.3 4.0 %gather_fusion = bf16[1024,512]{1,0:T(8,128)(2,1)S(1)} fusion(bf16[1024,512]{1,0:T(8,128)(2,1)S(1)} %copy-done, s32[1024]{0:T(1024)S(1)} %broadcast_clamp_fusion), kind=kCustom, calls=%fused_computation | custom fusion | bytes 2101248 | tf_op jit(solution)/shard_map/jit(_take)/gather | solution.py:68
  61.3 0.0 copy-done.1
  61.3 0.0 copy-done.2
  61.3 1.0 %select_convert_fusion = bf16[8,1,128,512]{3,2,1,0:T(8,128)(2,1)S(1)} fusion(f32[512]{0:T(512)S(1)} %mul.63, f32[512]{0:T(512)S(1)} %bitcast.115, bf16[8,1,128,512]{3,2,1,0:T(8,128)(2,1)S(1)} %bitcast.105, pred[8,128]{1,0:T(8,128)(4,1)S(1)} %compare_and_fusion, pred[8,128]{1,0:T(8,128)(4,1)S(1)} %get-tuple-element.205), kind=kLoop, calls=%fused_computation.15 | loop fusion | flops 3145728 | bytes 2103296 | tf_op jit(solution)/shard_map/convert_element_type | solution.py:70
  62.3 0.7 fusion.16
  62.9 0.7 fusion.15
  63.6 0.7 fusion.14
  64.3 0.7 fusion.13
  64.9 0.7 fusion.12
  65.6 0.7 fusion.11
  66.3 0.7 fusion.10
  66.9 0.7 fusion.9
  67.6 3.6 %all-to-all-start.2 = ((bf16[8,1,1,128,512]{4,3,2,1,0:T(8,128)(2,1)}), bf16[8,1,1,128,512]{4,3,2,1,0:T(8,128)(2,1)S(1)}, u32[]{:S(2)}, u32[]{:S(2)}) async-start(bf16[8,1,1,128,512]{4,3,2,1,0:T(8,128)(2,1)} %fusion.9), calls=%async_computation.2 | async-start | bytes 2097152 | tf_op jit(solution)/shard_map/all_to_all | solution.py:75
  71.2 0.6 pad_maximum_fusion
  71.7 21.2 %all-to-all-done.2 = bf16[8,1,1,128,512]{4,3,2,1,0:T(8,128)(2,1)S(1)} async-done(((bf16[8,1,1,128,512]{4,3,2,1,0:T(8,128)(2,1)}), bf16[8,1,1,128,512]{4,3,2,1,0:T(8,128)(2,1)S(1)}, u32[]{:S(2)}, u32[]{:S(2)}) %all-to-all-start.2) | async-done | bytes 1048608 | tf_op jit(solution)/shard_map/all_to_all | solution.py:75
  93.0 1.0 %copy.58 = bf16[1,8,128,512]{3,2,1,0:T(8,128)(2,1)} copy(bf16[1,8,128,512]{3,2,1,0:T(8,128)(2,1)S(1)} %bitcast.106) | data formatting | bytes 2097152
  (26 shorter events, 0.4 us)
Async XLA Ops:
  2.0 13.7 %all-to-all-start = ((s32[1,8,1]{2,0,1:T(1,128)}), s32[1,8,1]{2,0,1:T(1,128)S(1)}, u32[]{:S(2)}, u32[]{:S(2)}) async-start(s32[1,8,1]{2,0,1:T(1,128)} %copy.29), calls=%async_computation | async-start | bytes 8192 | tf_op jit(solution)/shard_map/all_to_all | solution.py:40
  11.6 2.0 %copy-start.3 = (u32[32]{0:T(128)S(1)}, u32[32]{0:T(128)}, u32[]{:S(2)}) copy-start(u32[32]{0:T(128)} %constant.87) | copy-start | bytes 388
  13.6 43.7 %copy-start = (bf16[1024,512]{1,0:T(8,128)(2,1)S(1)}, bf16[1024,512]{1,0:T(8,128)(2,1)}, u32[]{:S(2)}) copy-start(bf16[1024,512]{1,0:T(8,128)(2,1)} %param.8) | copy-start | bytes 3145732
  15.7 11.7 %all-to-all-start.1 = ((s32[1,8,128]{2,0,1:T(1,128)}), s32[1,8,128]{2,0,1:T(1,128)S(1)}, u32[]{:S(2)}, u32[]{:S(2)}) async-start(s32[1,8,128]{2,0,1:T(1,128)} %bitcast.4), calls=%async_computation.1 | async-start | bytes 8192 | tf_op jit(solution)/shard_map/all_to_all | solution.py:39
  33.1 28.2 %copy-start.1 = (s32[1024]{0:T(1024)}, s32[1024]{0:T(1024)S(1)}, u32[]{:S(2)}) copy-start(s32[1024]{0:T(1024)S(1)} %psum.7) | copy-start | bytes 12292
  57.3 4.0 %copy-start.2 = (f32[512]{0:T(512)S(1)}, f32[512]{0:T(512)}, u32[]{:S(2)}) copy-start(f32[512]{0:T(512)} %param.9) | copy-start | bytes 6148
  67.6 25.4 %all-to-all-start.2 = ((bf16[8,1,1,128,512]{4,3,2,1,0:T(8,128)(2,1)}), bf16[8,1,1,128,512]{4,3,2,1,0:T(8,128)(2,1)S(1)}, u32[]{:S(2)}, u32[]{:S(2)}) async-start(bf16[8,1,1,128,512]{4,3,2,1,0:T(8,128)(2,1)} %fusion.9), calls=%async_computation.2 | async-start | bytes 2097152 | tf_op jit(solution)/shard_map/all_to_all | solution.py:75
